TPU v7x, 32 devices: a whole 2x2x4 slice. The times are simulated.
32 devices in a mesh: dp: 4 (over y, core), expert: 4 (over z), tensor: 2 (over x).
Axes of the slice: x: 2, y: 2, z: 4, core: 2. Of those that a mesh axis runs over, the one named last changes fastest.
Arguments:
- router_input: bfloat16 [1024, 2048], P(('dp', 'expert'), 'tensor'), may hold values from -6 to 6
- router_weight: bfloat16 [2048, 8], replicated, may hold values from -0.125 to 0.125
- expert_ids: int32 [1024, 2], P(('dp', 'expert', 'tensor')), may hold values from 0 to 7, all different within a row; in each aligned block of 32 rows (0 to 31, 32 to 63, ...) at most 9 rows name the same one
- down_weight: bfloat16 [61440, 2048], P(('expert', 'tensor')), may hold values from -0.0625 to 0.0625
- hidden: bfloat16 [4, 72, 61440], P('dp', None, ('expert', 'tensor')), may hold values from -6 to 6
- grad_output: bfloat16 [1024, 2048], P(('dp', 'expert', 'tensor')), may hold values from -4 to 4
Outputs:
- weight_grad: bfloat16 [61440, 2048], P(('expert', 'tensor', 'dp'))
- hidden_grad: bfloat16 [4, 72, 61440], P('dp', None, ('expert', 'tensor'))
- router_grad: float32 [2048, 8], replicated
- input_grad: bfloat16 [1024, 2048], P(('dp', 'expert', 'tensor'))
Inputs may be any that keep to these rules, and one draw needn't show every extreme that they name: `expert_ids`: each row names 2 different experts. Within the 32 rows of one device no expert is named more than 9 times, and some device's rows name some expert exactly 9 times.
All inputs are finite; a program needn't handle non-finite values.
Results may differ from a plain program's by a relative error of at most 0.018.
Values may be sent and summed in bfloat16 or wider, within the bound.
A program may use at most 192 MiB of HBM per device.

v0:
```python
import jax
import jax.numpy as jnp
from jax import lax
from jax.sharding import PartitionSpec as P


def per_device(router_input, router_weight, expert_ids, down_weight, hidden, grad_output):
    token_rows = grad_output.shape[0]
    model_width = grad_output.shape[1]
    expert_count = router_weight.shape[1]
    choose_count = expert_ids.shape[1]
    expert_ranks = lax.axis_size("expert")
    tensor_ranks = lax.axis_size("tensor")
    sources = expert_ranks * tensor_ranks
    spread = sources // expert_count
    capacity = hidden.shape[1] // sources
    full_input = lax.all_to_all(router_input, "tensor", split_axis=0, concat_axis=1, tiled=True)
    logits = jnp.dot(full_input, router_weight, preferred_element_type=jnp.float32)
    labels = jnp.arange(expert_count, dtype=jnp.int32)
    onehot_int = (expert_ids[:, :, None] == labels).astype(jnp.int32)
    onehot = onehot_int.astype(jnp.float32)
    picked = jnp.sum(onehot * logits[:, None, :], axis=2)
    first_gate = jax.nn.sigmoid(picked[:, 0] - picked[:, 1])
    second_gate = jax.nn.sigmoid(picked[:, 1] - picked[:, 0])
    gate_values = jnp.stack([first_gate, second_gate], axis=1)
    gate_low = gate_values.astype(jnp.bfloat16)
    flat_hits = onehot_int.reshape(token_rows * choose_count, expert_count)
    before = jnp.cumsum(flat_hits, axis=0) - flat_hits
    slot_pos = jnp.sum(before * flat_hits, axis=1).reshape(token_rows, choose_count)
    slot_ids = jnp.arange(capacity, dtype=jnp.int32)
    dispatch_table = onehot[:, :, :, None] * (slot_pos[:, :, None, None] == slot_ids).astype(
        jnp.float32
    )
    slot_table = jnp.sum(dispatch_table, axis=1).astype(jnp.bfloat16)
    packed_grad = jnp.einsum(
        "rec,rd->ecd", slot_table, grad_output, preferred_element_type=jnp.float32
    ).astype(jnp.bfloat16)
    packed_gate = jnp.einsum("rkec,rk->ec", dispatch_table, gate_low.astype(jnp.float32)).astype(
        jnp.bfloat16
    )
    send_grad = jnp.repeat(packed_grad, spread, axis=0)
    send_gate = jnp.repeat(packed_gate, spread, axis=0)
    recv_grad, recv_gate = (
        lax.all_to_all(send_grad, ("expert", "tensor"), split_axis=0, concat_axis=0, tiled=True),
        lax.all_to_all(send_gate, ("expert", "tensor"), split_axis=0, concat_axis=0, tiled=True),
    )
    recv_grad = recv_grad.reshape(sources * capacity, model_width)
    recv_gate = recv_gate.reshape(sources * capacity).astype(jnp.float32)
    hidden_rows = hidden[0]
    gated_grad = (recv_gate[:, None] * recv_grad.astype(jnp.float32)).astype(jnp.bfloat16)
    expert_image = lax.dot_general(
        recv_grad, down_weight, (((1,), (1,)), ((), ())), preferred_element_type=jnp.float32
    )
    hidden_part = (recv_gate[:, None] * expert_image).astype(jnp.bfloat16)
    gate_partial = jnp.sum(hidden_rows.astype(jnp.float32) * expert_image, axis=1).reshape(
        sources, capacity
    )
    returned = lax.all_to_all(
        gate_partial, ("expert", "tensor"), split_axis=0, concat_axis=0, tiled=True
    )
    expert_sums = jnp.sum(returned.reshape(expert_count, spread, capacity), axis=1)
    gate_grad = jnp.einsum("rkec,ec->rk", dispatch_table, expert_sums)
    mixed_term = jnp.sum(gate_values * gate_grad, axis=1, keepdims=True)
    logit_part = gate_values * (gate_grad - mixed_term)
    logit_grad = jnp.sum(onehot * logit_part[:, :, None], axis=1)
    input_grad = jnp.dot(
        logit_grad, router_weight.astype(jnp.float32).T, precision=lax.Precision.HIGHEST
    ).astype(jnp.bfloat16)
    router_local = jnp.dot(
        full_input.astype(jnp.float32).T, logit_grad, precision=lax.Precision.HIGHEST
    )
    router_grad = lax.psum(router_local, ("dp", "expert", "tensor"))
    hidden_all = lax.all_to_all(hidden_rows, "dp", split_axis=1, concat_axis=0, tiled=True)
    gated_all = lax.all_gather(gated_grad, "dp", axis=0, tiled=True)
    weight_sum = lax.dot_general(
        hidden_all, gated_all, (((0,), (0,)), ((), ())), preferred_element_type=jnp.float32
    ).astype(jnp.bfloat16)
    return (weight_sum, hidden_part[None], router_grad, input_grad)


def solution(mesh):
    return jax.shard_map(
        per_device,
        mesh=mesh,
        in_specs=(
            P(("dp", "expert"), "tensor"),
            P(),
            P(("dp", "expert", "tensor"), None),
            P(("expert", "tensor"), None),
            P("dp", None, ("expert", "tensor")),
            P(("dp", "expert", "tensor"), None),
        ),
        out_specs=(
            P(("expert", "tensor", "dp"), None),
            P("dp", None, ("expert", "tensor")),
            P(),
            P(("dp", "expert", "tensor"), None),
        ),
        check_vma=False,
    )
```

profile of v0, /device:TPU:1, one launch (start us, length us, event | category | flops | bytes accessed | tf_op | source)
XLA Modules:
  0.0 211.5 jit_solution(2945085626296198110)
XLA Ops:
  8.0 3.5 %all-to-all-start = ((bf16[2,32,1024]{2,1,0:T(8,128)(2,1)}), bf16[2,32,1024]{2,1,0:T(8,128)(2,1)S(1)}, u32[]{:S(2)}, u32[]{:S(2)}) async-start(bf16[2,32,1024]{2,1,0:T(8,128)(2,1)} %bitcast.51), calls=%async_computation | async-start | bytes 262144 | tf_op jit(solution)/shard_map/all_to_all | solution.py:17
  11.5 0.8 copy.34
  13.7 1.7 all-to-all-done
  15.4 0.9 fusion.14
  16.3 0.7 multiply_reduce_fusion.2
  18.0 4.9 %all-to-all-start.1 = ((bf16[8,1,9]{2,1,0:T(2,128)(2,1)}), bf16[8,1,9]{2,1,0:T(2,128)(2,1)S(1)}, u32[]{:S(2)}, u32[]{:S(2)}) async-start(bf16[8,1,9]{2,1,0:T(2,128)(2,1)} %copy.37), calls=%async_computation.1 | async-start | bytes 8192 | tf_op jit(solution)/shard_map/all_to_all | solution.py:45
  22.8 1.1 convolution_convert_fusion
  23.9 4.2 %all-to-all-done.1 = bf16[8,1,9]{2,1,0:T(2,128)(2,1)S(1)} async-done(((bf16[8,1,9]{2,1,0:T(2,128)(2,1)}), bf16[8,1,9]{2,1,0:T(2,128)(2,1)S(1)}, u32[]{:S(2)}, u32[]{:S(2)}) %all-to-all-start.1) | async-done | bytes 176 | tf_op jit(solution)/shard_map/all_to_all | solution.py:45
  28.1 3.5 %all-to-all-start.2 = ((bf16[8,9,2048]{2,1,0:T(8,128)(2,1)}), bf16[8,9,2048]{2,1,0:T(8,128)(2,1)S(1)}, u32[]{:S(2)}, u32[]{:S(2)}) async-start(bf16[8,9,2048]{2,1,0:T(8,128)(2,1)} %convolution_convert_fusion), calls=%async_computation.2 | async-start | bytes 1048576 | tf_op jit(solution)/shard_map/all_to_all | solution.py:44
  31.7 10.3 %all-to-all-done.2 = bf16[8,9,2048]{2,1,0:T(8,128)(2,1)S(1)} async-done(((bf16[8,9,2048]{2,1,0:T(8,128)(2,1)}), bf16[8,9,2048]{2,1,0:T(8,128)(2,1)S(1)}, u32[]{:S(2)}, u32[]{:S(2)}) %all-to-all-start.2) | async-done | bytes 294944 | tf_op jit(solution)/shard_map/all_to_all | solution.py:44
  42.2 0.8 multiply_convert_fusion.1
  43.0 15.7 %fusion = (f32[72]{0:T(128)S(1)}, bf16[1,72,7680]{2,1,0:T(8,128)(2,1)}) fusion(bf16[1,72,7680]{2,1,0:T(8,128)(2,1)S(1)} %copy-done.1, f32[72]{0:T(128)S(1)} %reshape.61, bf16[72,2048]{1,0:T(8,128)(2,1)S(1)} %reshape.60, bf16[7680,2048]{1,0:T(8,128)(2,1)} %param.9), kind=kOutput, calls=%fused_computation.5 | convolution fusion | flops 2267688960 | bytes 33964608 | tf_op jit(solution)/shard_map/dot_general | solution.py:51
  58.8 0.7 all_to_all.54
  59.5 6.6 %all-to-all-start.4 = ((f32[8,1,9]{2,1,0:T(1,128)}), f32[8,1,9]{2,1,0:T(1,128)S(1)}, u32[]{:S(2)}, u32[]{:S(2)}) async-start(f32[8,1,9]{2,1,0:T(1,128)} %bitcast.13), calls=%async_computation.4 | async-start | bytes 8192 | tf_op jit(solution)/shard_map/all_to_all | solution.py:58
  66.4 1.1 copy.39
  67.5 3.8 %all-to-all-done.4 = f32[8,1,9]{2,1,0:T(1,128)S(1)} async-done(((f32[8,1,9]{2,1,0:T(1,128)}), f32[8,1,9]{2,1,0:T(1,128)S(1)}, u32[]{:S(2)}, u32[]{:S(2)}) %all-to-all-start.4) | async-done | bytes 320 | tf_op jit(solution)/shard_map/all_to_all | solution.py:58
  71.3 6.7 %all-to-all-start.3 = ((bf16[72,4,1920]{2,0,1:T(8,128)(2,1)}), bf16[72,4,1920]{2,0,1:T(8,128)(2,1)S(1)}, u32[]{:S(2)}, u32[]{:S(2)}) async-start(bf16[72,4,1920]{2,0,1:T(8,128)(2,1)} %copy.39), calls=%async_computation.3 | async-start | bytes 2211840 | tf_op jit(solution)/shard_map/all_to_all | solution.py:73
  78.2 0.8 convolution_bitcast_fusion
  79.1 1.0 convolution_convert_fusion.1
  80.0 12.1 %all-to-all-done.3 = bf16[72,4,1920]{2,0,1:T(8,128)(2,1)S(1)} async-done(((bf16[72,4,1920]{2,0,1:T(8,128)(2,1)}), bf16[72,4,1920]{2,0,1:T(8,128)(2,1)S(1)}, u32[]{:S(2)}, u32[]{:S(2)}) %all-to-all-start.3) | async-done | bytes 1105952 | tf_op jit(solution)/shard_map/all_to_all | solution.py:73
  92.1 8.0 %convert_bitcast_fusion = bf16[1920,2048]{0,1:T(8,128)(2,1)} fusion(bf16[288,2048]{1,0:T(8,128)(2,1)} %all-gather.2.cloned.1.call-done, bf16[288,1920]{1,0:T(8,128)(2,1)S(1)} %bitcast.49), kind=kOutput, calls=%fused_computation | convolution fusion | flops 2268856320 | bytes 10149888 | tf_op jit(solution)/shard_map/dot_general | solution.py:75
  100.1 10.6 %copy.41 = bf16[1920,2048]{1,0:T(8,128)(2,1)} copy(bf16[1920,2048]{0,1:T(8,128)(2,1)} %convert_bitcast_fusion) | data formatting | bytes 15728640
  110.7 91.9 %all-reduce.2.cloned.1.call-done = f32[2048,8]{0,1:T(8,128)} async-done(((f32[2048,8]{0,1:T(8,128)}), f32[2048,8]{0,1:T(8,128)}) %all-reduce.2.cloned.1.call-update) | async-done | bytes 65552 | tf_op jit(solution)/shard_map/psum | solution.py:72
  202.5 1.5 copy.56
  (38 shorter events, 3.2 us)
Async XLA Ops:
  8.0 14.8 %copy-start = (bf16[32,2048]{1,0:T(8,128)(2,1)S(1)}, bf16[32,2048]{1,0:T(8,128)(2,1)}, u32[]{:S(2)}) copy-start(bf16[32,2048]{1,0:T(8,128)(2,1)} %param.11) | copy-start | bytes 393220
  8.0 7.4 %all-to-all-start = ((bf16[2,32,1024]{2,1,0:T(8,128)(2,1)}), bf16[2,32,1024]{2,1,0:T(8,128)(2,1)S(1)}, u32[]{:S(2)}, u32[]{:S(2)}) async-start(bf16[2,32,1024]{2,1,0:T(8,128)(2,1)} %bitcast.51), calls=%async_computation | async-start | bytes 262144 | tf_op jit(solution)/shard_map/all_to_all | solution.py:17
  18.0 10.1 %all-to-all-start.1 = ((bf16[8,1,9]{2,1,0:T(2,128)(2,1)}), bf16[8,1,9]{2,1,0:T(2,128)(2,1)S(1)}, u32[]{:S(2)}, u32[]{:S(2)}) async-start(bf16[8,1,9]{2,1,0:T(2,128)(2,1)} %copy.37), calls=%async_computation.1 | async-start | bytes 8192 | tf_op jit(solution)/shard_map/all_to_all | solution.py:45
  23.9 19.1 %copy-start.1 = (bf16[1,72,7680]{2,1,0:T(8,128)(2,1)S(1)}, bf16[1,72,7680]{2,1,0:T(8,128)(2,1)}, u32[]{:S(2)}) copy-start(bf16[1,72,7680]{2,1,0:T(8,128)(2,1)} %param.10) | copy-start | bytes 3317764
  28.1 13.9 %all-to-all-start.2 = ((bf16[8,9,2048]{2,1,0:T(8,128)(2,1)}), bf16[8,9,2048]{2,1,0:T(8,128)(2,1)S(1)}, u32[]{:S(2)}, u32[]{:S(2)}) async-start(bf16[8,9,2048]{2,1,0:T(8,128)(2,1)} %convolution_convert_fusion), calls=%async_computation.2 | async-start | bytes 1048576 | tf_op jit(solution)/shard_map/all_to_all | solution.py:44
  31.6 60.5 %all-gather.2.cloned.1.call-start = ((), (), s32[]{:S(2)}) async-start(), calls=%async_computation.5 | async-start | bytes 1474560 | tf_op jit(solution)/shard_map/all_gather | solution.py:74
  59.5 11.9 %all-to-all-start.4 = ((f32[8,1,9]{2,1,0:T(1,128)}), f32[8,1,9]{2,1,0:T(1,128)S(1)}, u32[]{:S(2)}, u32[]{:S(2)}) async-start(f32[8,1,9]{2,1,0:T(1,128)} %bitcast.13), calls=%async_computation.4 | async-start | bytes 8192 | tf_op jit(solution)/shard_map/all_to_all | solution.py:58
  67.5 10.7 %copy-start.3 = (s32[32,2]{0,1:T(2,128)S(1)}, s32[32,2]{0,1:T(2,128)}, u32[]{:S(2)}) copy-start(s32[32,2]{0,1:T(2,128)} %param.8) | copy-start | bytes 772
  67.5 11.6 %copy-start.2 = (bf16[2048,8]{0,1:T(8,128)(2,1)S(1)}, bf16[2048,8]{0,1:T(8,128)(2,1)}, u32[]{:S(2)}) copy-start(bf16[2048,8]{0,1:T(8,128)(2,1)} %param.7) | copy-start | bytes 98308
  71.3 20.8 %all-to-all-start.3 = ((bf16[72,4,1920]{2,0,1:T(8,128)(2,1)}), bf16[72,4,1920]{2,0,1:T(8,128)(2,1)S(1)}, u32[]{:S(2)}, u32[]{:S(2)}) async-start(bf16[72,4,1920]{2,0,1:T(8,128)(2,1)} %copy.39), calls=%async_computation.3 | async-start | bytes 2211840 | tf_op jit(solution)/shard_map/all_to_all | solution.py:73
  78.0 124.6 %all-reduce.2.cloned.1.call-start = ((), (), s32[]{:S(2)}) async-start(), calls=%async_computation.6 | async-start | bytes 131072 | tf_op jit(solution)/shard_map/psum | solution.py:72
Sparse Core Ops, SparseCore 0:
  43.1 21.1 all-gather.1
Sparse Core Ops, SparseCore 1:
  84.6 117.9 all-reduce.1
where the time goes:
time: 212 us; the launch traced here: 211 us
  waiting for transfers between devices  124 us (58%)
  matrix products  27.6 us (13%)
  starting transfers between devices  25.2 us (12%)
  local copies, waits for them, and re-layouts  16.3 us (8%)
  between operations  15.6 us (7%)
  other arithmetic  2.78 us (1%)
    psum x1, waiting for transfers between devices, per_device(): router_grad = lax.psum(router_local, ('dp', 'expert', 'tensor'))  91.9 us
    dot_general x1, matrix products, per_device(): lax.dot_general(recv_grad, down_weight, (((1,), (1,)), ((), ())), preferr...  15.7 us
    unnamed x12, local copies, waits for them, and re-layouts  13 us
    all_to_all x1, waiting for transfers between devices, per_device(): lax.all_to_all(hidden_rows, 'dp', split_axis=1, concat_axis=0, tiled=True)  12.1 us
    all_to_all x1, waiting for transfers between devices, per_device(): lax.all_to_all(send_grad, ('expert', 'tensor'), split_axis=0, concat_axis...  10.3 us
    dot_general x1, matrix products, per_device(): lax.dot_general(hidden_all, gated_all, (((0,), (0,)), ((), ())), preferre...  7.96 us
    all_to_all x1, starting transfers between devices, per_device(): lax.all_to_all(hidden_rows, 'dp', split_axis=1, concat_axis=0, tiled=True)  6.66 us
    all_to_all x1, starting transfers between devices, per_device(): lax.all_to_all(gate_partial, ('expert', 'tensor'), split_axis=0, concat_a...  6.6 us
  transfers between devices with their start and end apart: 7, of which 6 were waited for; matrix products, arithmetic and copies ran while one was open for 19% of the time, Pallas kernels for 0%

commit v1 on v0

--- a/solution.py
+++ b/solution.py
@@ -70,7 +70,9 @@
         full_input.astype(jnp.float32).T, logit_grad, precision=lax.Precision.HIGHEST
     )
     router_grad = lax.psum(router_local, ("dp", "expert", "tensor"))
-    hidden_all = lax.all_to_all(hidden_rows, "dp", split_axis=1, concat_axis=0, tiled=True)
+    cells = jnp.split(hidden_rows, lax.axis_size("dp"), axis=1)
+    arrived = lax.all_to_all(jnp.stack(cells), "dp", 0, 0)
+    hidden_all = jnp.concatenate(arrived, axis=0)
     gated_all = lax.all_gather(gated_grad, "dp", axis=0, tiled=True)
     weight_sum = lax.dot_general(
         hidden_all, gated_all, (((0,), (0,)), ((), ())), preferred_element_type=jnp.float32

time: 212 us -> 212 us (level)
  local copies, waits for them, and re-layouts: 16.3 us -> 4.34 us
  waiting for transfers between devices: 124 us -> 135 us
    psum x1, waiting for transfers between devices: 91.9 us -> 103 us  [per_device(): router_grad = lax.psum(router_local, ('dp', 'expert', 'tensor'))]
    unnamed x12 -> x11, local copies, waits for them, and re-layouts: 13 us -> 2.34 us
  transfers between devices with their start and end apart: 7 -> 7, of which waited for: 6 -> 6; matrix products, arithmetic and copies ran while one was open for 19% -> 14% of each run, Pallas kernels for 0% -> 0%
where the time goes in v1:
time: 212 us
  waiting for transfers between devices  135 us (64%)
  matrix products  27.2 us (13%)
  starting transfers between devices  25.2 us (12%)
  between operations  15.6 us (7%)
  local copies, waits for them, and re-layouts  4.34 us (2%)
  other arithmetic  3.95 us (2%)
    psum x1, waiting for transfers between devices, per_device(): router_grad = lax.psum(router_local, ('dp', 'expert', 'tensor'))  103 us
    dot_general x1, matrix products, per_device(): lax.dot_general(recv_grad, down_weight, (((1,), (1,)), ((), ())), preferr...  15.7 us
    all_to_all x1, waiting for transfers between devices, per_device(): arrived = lax.all_to_all(jnp.stack(cells), 'dp', 0, 0)  12.1 us
    all_to_all x1, waiting for transfers between devices, per_device(): lax.all_to_all(send_grad, ('expert', 'tensor'), split_axis=0, concat_axis...  10.2 us
    dot_general x1, matrix products, per_device(): lax.dot_general(hidden_all, gated_all, (((0,), (0,)), ((), ())), preferre...  7.47 us
    all_to_all x1, starting transfers between devices, per_device(): arrived = lax.all_to_all(jnp.stack(cells), 'dp', 0, 0)  6.66 us
    all_to_all x1, starting transfers between devices, per_device(): lax.all_to_all(gate_partial, ('expert', 'tensor'), split_axis=0, concat_a...  6.6 us
    all_to_all x1, starting transfers between devices, per_device(): lax.all_to_all(send_gate, ('expert', 'tensor'), split_axis=0, concat_axis...  4.86 us
  transfers between devices with their start and end apart: 7, of which 6 were waited for; matrix products, arithmetic and copies ran while one was open for 14% of the time, Pallas kernels for 0%

profile of v1, /device:TPU:1, one launch (start us, length us, event | category | flops | bytes accessed | tf_op | source)
XLA Modules:
  0.0 211.6 jit_solution(4608438540375382982)
XLA Ops:
  8.0 3.5 %all-to-all-start.1 = ((bf16[2,32,1024]{2,1,0:T(8,128)(2,1)}), bf16[2,32,1024]{2,1,0:T(8,128)(2,1)S(1)}, u32[]{:S(2)}, u32[]{:S(2)}) async-start(bf16[2,32,1024]{2,1,0:T(8,128)(2,1)} %bitcast.55), calls=%async_computation.1 | async-start | bytes 262144 | tf_op jit(solution)/shard_map/all_to_all | solution.py:17
  11.5 0.8 copy.24
  12.3 0.7 convert_convert_fusion
  13.7 1.7 all-to-all-done.1
  15.4 1.0 fusion.13
  16.4 0.7 multiply_reduce_fusion.3
  18.1 4.9 %all-to-all-start.2 = ((bf16[8,1,9]{2,1,0:T(2,128)(2,1)}), bf16[8,1,9]{2,1,0:T(2,128)(2,1)S(1)}, u32[]{:S(2)}, u32[]{:S(2)}) async-start(bf16[8,1,9]{2,1,0:T(2,128)(2,1)} %copy.27), calls=%async_computation.2 | async-start | bytes 8192 | tf_op jit(solution)/shard_map/all_to_all | solution.py:45
  22.9 1.1 convolution_convert_fusion.1
  24.0 4.2 %all-to-all-done.2 = bf16[8,1,9]{2,1,0:T(2,128)(2,1)S(1)} async-done(((bf16[8,1,9]{2,1,0:T(2,128)(2,1)}), bf16[8,1,9]{2,1,0:T(2,128)(2,1)S(1)}, u32[]{:S(2)}, u32[]{:S(2)}) %all-to-all-start.2) | async-done | bytes 176 | tf_op jit(solution)/shard_map/all_to_all | solution.py:45
  28.2 3.5 %all-to-all-start.3 = ((bf16[8,9,2048]{2,1,0:T(8,128)(2,1)}), bf16[8,9,2048]{2,1,0:T(8,128)(2,1)S(1)}, u32[]{:S(2)}, u32[]{:S(2)}) async-start(bf16[8,9,2048]{2,1,0:T(8,128)(2,1)} %convolution_convert_fusion.1), calls=%async_computation.3 | async-start | bytes 1048576 | tf_op jit(solution)/shard_map/all_to_all | solution.py:44
  32.0 10.2 %all-to-all-done.3 = bf16[8,9,2048]{2,1,0:T(8,128)(2,1)S(1)} async-done(((bf16[8,9,2048]{2,1,0:T(8,128)(2,1)}), bf16[8,9,2048]{2,1,0:T(8,128)(2,1)S(1)}, u32[]{:S(2)}, u32[]{:S(2)}) %all-to-all-start.3) | async-done | bytes 294944 | tf_op jit(solution)/shard_map/all_to_all | solution.py:44
  42.3 0.8 multiply_convert_fusion.1
  43.1 15.7 %multiply_reduce_fusion = (f32[72]{0:T(128)S(1)}, bf16[1,72,7680]{2,1,0:T(8,128)(2,1)}) fusion(bf16[1,72,7680]{2,1,0:T(8,128)(2,1)S(1)} %copy-done.1, f32[72]{0:T(128)S(1)} %reshape.59, bf16[72,2048]{1,0:T(8,128)(2,1)S(1)} %reshape.58, bf16[7680,2048]{1,0:T(8,128)(2,1)} %param.9), kind=kOutput, calls=%fused_computation.4 | convolution fusion | flops 2267688960 | bytes 33964608 | tf_op jit(solution)/shard_map/dot_general | solution.py:51
  58.9 0.7 all_to_all.40
  59.6 6.6 %all-to-all-start.4 = ((f32[8,1,9]{2,1,0:T(1,128)}), f32[8,1,9]{2,1,0:T(1,128)S(1)}, u32[]{:S(2)}, u32[]{:S(2)}) async-start(f32[8,1,9]{2,1,0:T(1,128)} %bitcast.15), calls=%async_computation.4 | async-start | bytes 8192 | tf_op jit(solution)/shard_map/all_to_all | solution.py:58
  66.2 1.2 pad_maximum_fusion
  67.3 4.1 %all-to-all-done.4 = f32[8,1,9]{2,1,0:T(1,128)S(1)} async-done(((f32[8,1,9]{2,1,0:T(1,128)}), f32[8,1,9]{2,1,0:T(1,128)S(1)}, u32[]{:S(2)}, u32[]{:S(2)}) %all-to-all-start.4) | async-done | bytes 320 | tf_op jit(solution)/shard_map/all_to_all | solution.py:58
  71.4 6.7 %all-to-all-start = ((bf16[4,72,1920]{2,1,0:T(8,128)(2,1)}), bf16[4,72,1920]{2,1,0:T(8,128)(2,1)S(1)}, u32[]{:S(2)}, u32[]{:S(2)}) async-start(bf16[4,72,1920]{2,1,0:T(8,128)(2,1)} %pad_maximum_fusion), calls=%async_computation | async-start | bytes 2211840 | tf_op jit(solution)/shard_map/all_to_all | solution.py:74
  78.3 0.8 convolution_bitcast_fusion
  79.2 1.0 convolution_convert_fusion.2
  80.1 12.1 %all-to-all-done = bf16[4,72,1920]{2,1,0:T(8,128)(2,1)S(1)} async-done(((bf16[4,72,1920]{2,1,0:T(8,128)(2,1)}), bf16[4,72,1920]{2,1,0:T(8,128)(2,1)S(1)}, u32[]{:S(2)}, u32[]{:S(2)}) %all-to-all-start) | async-done | bytes 1105952 | tf_op jit(solution)/shard_map/all_to_all | solution.py:74
  92.2 7.5 %convolution_convert_fusion = bf16[1920,2048]{1,0:T(8,128)(2,1)} fusion(bf16[288,1920]{1,0:T(8,128)(2,1)S(1)} %bitcast.53, bf16[288,2048]{1,0:T(8,128)(2,1)} %all-gather.2.cloned.1.call-done), kind=kOutput, calls=%fused_computation | convolution fusion | flops 2268856320 | bytes 10149888 | tf_op jit(solution)/shard_map/dot_general | solution.py:77
  99.7 103.0 %all-reduce.2.cloned.1.call-done = f32[2048,8]{0,1:T(8,128)} async-done(((f32[2048,8]{0,1:T(8,128)}), f32[2048,8]{0,1:T(8,128)}) %all-reduce.2.cloned.1.call-update) | async-done | bytes 65552 | tf_op jit(solution)/shard_map/psum | solution.py:72
  202.6 1.5 copy.44
  (37 shorter events, 2.2 us)
Async XLA Ops:
  8.0 14.9 %copy-start = (bf16[32,2048]{1,0:T(8,128)(2,1)S(1)}, bf16[32,2048]{1,0:T(8,128)(2,1)}, u32[]{:S(2)}) copy-start(bf16[32,2048]{1,0:T(8,128)(2,1)} %param.11) | copy-start | bytes 393220
  8.0 7.4 %all-to-all-start.1 = ((bf16[2,32,1024]{2,1,0:T(8,128)(2,1)}), bf16[2,32,1024]{2,1,0:T(8,128)(2,1)S(1)}, u32[]{:S(2)}, u32[]{:S(2)}) async-start(bf16[2,32,1024]{2,1,0:T(8,128)(2,1)} %bitcast.55), calls=%async_computation.1 | async-start | bytes 262144 | tf_op jit(solution)/shard_map/all_to_all | solution.py:17
  15.4 16.3 %copy-start.1 = (bf16[1,72,7680]{2,1,0:T(8,128)(2,1)S(1)}, bf16[1,72,7680]{2,1,0:T(8,128)(2,1)}, u32[]{:S(2)}) copy-start(bf16[1,72,7680]{2,1,0:T(8,128)(2,1)} %param.10) | copy-start | bytes 3317764
  18.1 10.1 %all-to-all-start.2 = ((bf16[8,1,9]{2,1,0:T(2,128)(2,1)}), bf16[8,1,9]{2,1,0:T(2,128)(2,1)S(1)}, u32[]{:S(2)}, u32[]{:S(2)}) async-start(bf16[8,1,9]{2,1,0:T(2,128)(2,1)} %copy.27), calls=%async_computation.2 | async-start | bytes 8192 | tf_op jit(solution)/shard_map/all_to_all | solution.py:45
  28.2 13.9 %all-to-all-start.3 = ((bf16[8,9,2048]{2,1,0:T(8,128)(2,1)}), bf16[8,9,2048]{2,1,0:T(8,128)(2,1)S(1)}, u32[]{:S(2)}, u32[]{:S(2)}) async-start(bf16[8,9,2048]{2,1,0:T(8,128)(2,1)} %convolution_convert_fusion.1), calls=%async_computation.3 | async-start | bytes 1048576 | tf_op jit(solution)/shard_map/all_to_all | solution.py:44
  31.7 60.5 %all-gather.2.cloned.1.call-start = ((), (), s32[]{:S(2)}) async-start(), calls=%async_computation.5 | async-start | bytes 1474560 | tf_op jit(solution)/shard_map/all_gather | solution.py:76
  59.6 11.9 %all-to-all-start.4 = ((f32[8,1,9]{2,1,0:T(1,128)}), f32[8,1,9]{2,1,0:T(1,128)S(1)}, u32[]{:S(2)}, u32[]{:S(2)}) async-start(f32[8,1,9]{2,1,0:T(1,128)} %bitcast.15), calls=%async_computation.4 | async-start | bytes 8192 | tf_op jit(solution)/shard_map/all_to_all | solution.py:58
  67.3 11.0 %copy-start.3 = (s32[32,2]{0,1:T(2,128)S(1)}, s32[32,2]{0,1:T(2,128)}, u32[]{:S(2)}) copy-start(s32[32,2]{0,1:T(2,128)} %param.8) | copy-start | bytes 772
  67.3 11.8 %copy-start.2 = (bf16[2048,8]{0,1:T(8,128)(2,1)S(1)}, bf16[2048,8]{0,1:T(8,128)(2,1)}, u32[]{:S(2)}) copy-start(bf16[2048,8]{0,1:T(8,128)(2,1)} %param.7) | copy-start | bytes 98308
  71.4 20.8 %all-to-all-start = ((bf16[4,72,1920]{2,1,0:T(8,128)(2,1)}), bf16[4,72,1920]{2,1,0:T(8,128)(2,1)S(1)}, u32[]{:S(2)}, u32[]{:S(2)}) async-start(bf16[4,72,1920]{2,1,0:T(8,128)(2,1)} %pad_maximum_fusion), calls=%async_computation | async-start | bytes 2211840 | tf_op jit(solution)/shard_map/all_to_all | solution.py:74
  78.1 124.6 %all-reduce.2.cloned.1.call-start = ((), (), s32[]{:S(2)}) async-start(), calls=%async_computation.6 | async-start | bytes 131072 | tf_op jit(solution)/shard_map/psum | solution.py:72
Sparse Core Ops, SparseCore 0:
  43.3 21.1 all-gather.1
Sparse Core Ops, SparseCore 1:
  84.7 117.9 all-reduce.1
